TPU v7x, 256 devices: a whole 4x4x8 slice. The times are simulated.
256 devices in a mesh: tower: 8 (over x, z_hi), px: 4 (over y), py: 8 (over z_lo, core).
Axes of the slice: x: 4, y: 4, z: 8 (z_hi: 2, z_lo: 4; z = z_hi * 4 + z_lo), core: 2. Of those that a mesh axis runs over, the one named last changes fastest.
Arguments:
- positions: float32 [3, 16, 8, 16, 128], P(None, 'tower', 'px', 'py'), may hold values from 0 to 1
- velocities: float32 [3, 16, 8, 16, 128], P(None, 'tower', 'px', 'py'), may hold values from -6 to 6
- types: int32 [16, 8, 16, 128], P('tower', 'px', 'py'), may hold values from 0 to 15
- strength: float32 [16], replicated, may hold values from 0.5 to 2
- counts: int32 [16, 8, 16], P('tower', 'px', 'py'), may hold values from 64 to 128
- pair_list: int32 [27, 16, 8, 16], P(None, 'tower', 'px', 'py'), may hold values from 0 to 1, as said below
- destination: int32 [16, 8, 16], P('tower', 'px', 'py'), may hold values from 0 to 3839, as said below
Outputs:
- moved_positions: float32 [3, 3840, 128], P(None, ('tower', 'px', 'py'))
- moved_velocities: float32 [3, 3840, 128], P(None, ('tower', 'px', 'py'))
Inputs may be any that keep to these rules, and one draw needn't show every extreme that they name: pair_list[k] at cell c equals pair_list[26 - k] at the cell c plus the offset of k. `destination`: the values are distinct; a block's slot lies among the 15 slots (slot // 15 names a device, numbered tower-major, then px, then py) of a device with the same tower index and the same px index as the block's owner; from each device either no block or exactly 2 blocks go to other devices, at most 1 of them to any one device; among the devices of one tower index and one px index, one device receives exactly 1 block from every other and holds exactly 15 blocks afterwards.
All inputs are finite; a program needn't handle non-finite values.
Results may differ from a plain program's by a relative error of at most 0.0001.
Values sent between devices are 32-bit elements; how exact they have to be, the bound alone decides.
A program may use at most 64 MiB of HBM per device.

v0:
```python
import itertools

import jax
import jax.numpy as jnp
from jax import lax
from jax.experimental import pallas as pl
from jax.experimental.pallas import tpu as pltpu
from jax.sharding import PartitionSpec as P

STEPS = 4
STEP_TIME = 0.02
KINDS = 16
SEATS = 15
ATOMS = 128
DEPTH = 192
MESH = pl.DeviceIdType.MESH
F32 = jnp.float32
BF16 = jnp.bfloat16

DIRECTIONS = sorted(
    (d for d in itertools.product((-1, 0, 1), repeat=3) if d != (0, 0, 0)),
    key=lambda d: abs(d[0]),
)
NEAR = 8
SEAT_OF_Y = {0: 0, 1: 1, -1: 2, 2: 3}


def spans(step):
    if step == 0:
        return pl.ds(1, 2), pl.ds(1, 2)
    return (pl.ds(2, 1), pl.ds(0, 1)) if step == 1 else (pl.ds(1, 1), pl.ds(3, 1))


def spans_y(step):
    if step == 0:
        return pl.ds(0, 2), pl.ds(0, 2)
    return (pl.ds(1, 1), pl.ds(2, 1)) if step == 1 else (pl.ds(0, 1), pl.ds(3, 1))


def thirds(x):
    high = x.astype(BF16).astype(F32)
    rest = x - high
    mid = rest.astype(BF16).astype(F32)
    return high, mid, rest - mid


def swap_halves(x):
    return jnp.concatenate([x[4:], x[:4]], axis=0)


def body(
    pos_ref, vel_ref, types_ref, strength_ref, counts_ref, pair_ref, dest_ref,
    out_pos_ref, out_vel_ref,
    region, speed, live_ref, flag_ref, left_ref, right_ref, value_ref, total, box, send_box,
    send_sem, recv_sem, move_send_sem, move_recv_sem,
):
    me_z, me_x, me_y = (lax.axis_index(a) for a in ("tower", "px", "py"))
    n_z, n_x, n_y = (lax.axis_size(a) for a in ("tower", "px", "py"))

    def device(d):
        return (
            lax.rem(me_z + d[0] + n_z, n_z),
            lax.rem(me_x + d[1] + n_x, n_x),
            lax.rem(me_y + d[2] + n_y, n_y),
        )

    peers = [(0, 0, r) for r in range(1, 8)]
    greeted = DIRECTIONS + [p for p in peers if p[2] not in (1, 7)]
    barrier = pltpu.get_barrier_semaphore()
    for d in greeted:
        pl.semaphore_signal(barrier, inc=1, device_id=device(d), device_id_type=MESH)

    row8 = lax.broadcasted_iota(jnp.int32, (8, ATOMS), 0)
    low = row8 < 4
    comp = lax.rem(row8, 4)
    is_xyz = comp < 3
    zero8 = jnp.zeros((8, ATOMS), F32)

    kinds = types_ref[...].reshape(8, ATOMS)
    table = jnp.zeros((8, ATOMS), F32)
    for kind in range(KINDS):
        table = jnp.where(kinds == kind, strength_ref[kind], table)
    lanes = lax.broadcasted_iota(jnp.int32, (1, ATOMS), 1)
    for cell in range(8):
        z, x, y = cell // 4, cell // 2 % 2, cell % 2
        live = (lanes < counts_ref[z, x, y]).astype(F32)
        live_ref[pl.ds(cell, 1), :] = live
        for k in range(3):
            region[0, 1 + z, 1 + x, y, pl.ds(k, 1), :] = pos_ref[k, z, x, pl.ds(y, 1), :]
            speed[cell // 2, pl.ds(4 * y + k, 1), :] = vel_ref[k, z, x, pl.ds(y, 1), :]
        region[0, 1 + z, 1 + x, y, pl.ds(3, 1), :] = table[cell : cell + 1] * live
        speed[cell // 2, pl.ds(4 * y + 3, 1), :] = jnp.zeros((1, ATOMS), F32)

    def halo_copies(slot):
        copies = []
        for i, d in enumerate(DIRECTIONS):
            (sz, tz), (sx, tx), (sy, ty) = spans(d[0]), spans(d[1]), spans_y(d[2])
            copies.append(
                pltpu.make_async_remote_copy(
                    src_ref=region.at[slot, sz, sx, sy],
                    dst_ref=region.at[slot, tz, tx, ty],
                    send_sem=send_sem.at[slot, i],
                    recv_sem=recv_sem.at[slot, i],
                    device_id=device(d),
                    device_id_type=MESH,
                )
            )
        return copies

    def static_parts():
        for z, x in itertools.product(range(4), range(4)):
            tiles = []
            for y in (0, 1, -1, 2):
                tile = zero8
                for cell in range(8):
                    o = (z - 1 - cell // 4, x - 1 - cell // 2 % 2, y - cell % 2)
                    if max(map(abs, o)) <= 1:
                        k = (o[0] + 1) * 9 + (o[1] + 1) * 3 + o[2] + 1
                        flag = pair_ref[k, cell // 4, cell // 2 % 2, cell % 2]
                        tile = jnp.where(row8 == cell, (flag.astype(F32) - 1.0) * 100.0, tile)
                tiles.append(tile)
            flag_ref[4 * z + x] = jnp.concatenate(tiles, axis=0).astype(BF16)
        for p in range(4):
            for t in range(3):
                for side in range(2):
                    half = ((0, 0), (1, 1), (0, 1))[t][side]
                    mark = jnp.where((low if half == 0 else ~low) & is_xyz, -1.0, 0.0)
                    pair = [mark, zero8] if t < 2 else [zero8, mark]
                    seat = ((0, 0), (1, 1), (2, 3))[t][side]
                    picks = [
                        jnp.where(row8 == 2 * p + side, 1.0, 0.0) if s == seat else zero8
                        for s in range(4)
                    ]
                    right_ref[p, t, 96:144, pl.ds(128 * side, 128)] = jnp.concatenate(
                        pair * 3, axis=0
                    ).astype(BF16)
                    right_ref[p, t, 160:192, pl.ds(128 * side, 128)] = jnp.concatenate(
                        picks, axis=0
                    ).astype(BF16)

    def shift_of(z, x, part):
        y_low, y_high = ((-1.0, 0.0), (-2.0, 1.0))[part]
        y = jnp.where(low, y_low, y_high)
        return jnp.where(
            comp == 0, z - 2.0, jnp.where(comp == 1, x - 2.0, jnp.where(comp == 2, y, 0.0))
        )

    def own_tile(slot, z, x, part):
        return jnp.concatenate(
            [region[slot, z, x, 2 * part], region[slot, z, x, 2 * part + 1]], axis=0
        )

    def strength_rows(tile):
        return jnp.concatenate(
            [
                jnp.broadcast_to(tile[3:4], (4, ATOMS)),
                jnp.broadcast_to(tile[7:8], (4, ATOMS)),
            ],
            axis=0,
        )

    def build_left(slot, z, x, both):
        column = 4 * z + x
        parts = []
        for part in range(2):
            if part == 1 and not both:
                parts.append([zero8] * 6)
                continue
            raw = own_tile(slot, z, x, part)
            tile = raw + shift_of(z, x, part)
            parts.append(list(thirds(tile)) + list(thirds(tile * tile)))
            value = jnp.where(is_xyz, tile, 1.0) * strength_rows(raw)
            high = value.astype(BF16).astype(F32)
            value_ref[part, :, pl.ds(128 * column, 128)] = jnp.concatenate(
                [high, value - high], axis=0
            ).astype(BF16)
        rows = []
        for kind in (0, 0, 1, 1, 0, 2, 3, 4, 5):
            rows += [parts[0][kind], parts[1][kind]]
        rows += [jnp.ones((16, ATOMS), F32)]
        stack = jnp.concatenate(
            [jnp.concatenate(rows, axis=0).astype(BF16), flag_ref[column]], axis=0
        )
        left_ref[column] = stack.T

    def build_right(slot):
        for p in range(4):
            z, x = 1 + p // 2, 1 + p % 2
            tile = own_tile(slot, z, x, 0) + shift_of(z, x, 0)
            tile = jnp.where(is_xyz, tile, 0.0)
            high, mid, rest = (2.0 * v for v in thirds(tile))
            terms = [high, mid, high, mid, rest, high]
            swapped = [swap_halves(v) for v in (high, mid, rest)]
            swapped = [swapped[i] for i in (0, 1, 0, 1, 2, 0)]
            squares = [-v for v in thirds(tile * tile)]
            squares_swapped = [swap_halves(v) for v in squares]
            for side in range(2):
                a, b = (squares, squares_swapped) if side == 0 else (squares_swapped, squares)
                ones_rows = jnp.concatenate(
                    [
                        jnp.where(low, jnp.where(is_xyz, a[0], 1.0), b[1]),
                        jnp.where(low, a[2], 0.0),
                    ],
                    axis=0,
                ).astype(BF16)
                for t in range(3):
                    half = ((0, 0), (1, 1), (0, 1))[t][side]
                    source = terms if half == side else swapped
                    keep = low if half == 0 else ~low
                    rows = []
                    for v in source:
                        v = jnp.where(keep, v, 0.0)
                        rows += [v, zero8] if t < 2 else [zero8, v]
                    at = pl.ds(128 * side, 128)
                    right_ref[p, t, 0:96, at] = jnp.concatenate(rows, axis=0).astype(BF16)
                    right_ref[p, t, 144:160, at] = ones_rows

    def add_pairs(p, t, columns, first):
        lhs = jnp.concatenate([left_ref[c] for c in columns], axis=0)
        near = jnp.dot(lhs, right_ref[p, t], preferred_element_type=F32)
        near = jnp.maximum(near, 0.0)
        weight = near * near
        high = weight.astype(BF16)
        rest = (weight - high.astype(F32)).astype(BF16)
        part = 0 if t < 2 else 1
        values = jnp.concatenate(
            [value_ref[part, :, pl.ds(128 * c, 128)] for c in columns], axis=1
        )
        add = jnp.dot(values, high, preferred_element_type=F32) + jnp.dot(
            values, rest, preferred_element_type=F32
        )
        if first:
            total[p, t] = add
        else:
            total[p, t] += add

    def update(slot):
        for p in range(4):
            z, x = 1 + p // 2, 1 + p % 2
            both = total[p, 0]
            both = both[:8] + both[8:]
            other = total[p, 1]
            other = other[:8] + other[8:]
            apart = total[p, 2]
            apart = apart[:8] + apart[8:]
            sums = jnp.concatenate(
                [
                    both[:4, :128] + other[4:, :128] + apart[:4, :128],
                    both[:4, 128:] + other[4:, 128:] + apart[4:, 128:],
                ],
                axis=0,
            )
            raw = own_tile(slot, z, x, 0)
            tile = raw + shift_of(z, x, 0)
            force = -6.0 * strength_rows(raw) * (sums - tile * strength_rows(sums))
            new_speed = speed[p] + STEP_TIME * jnp.where(is_xyz, force, 0.0)
            speed[p] = new_speed
            new = raw + STEP_TIME * new_speed
            region[slot + 1, z, x, 0] = new[:4]
            region[slot + 1, z, x, 1] = new[4:]

    own = [(z, x) for z in (1, 2) for x in (1, 2)]

    def one_step(slot, carry):
        copies = halo_copies(slot)
        for copy in copies:
            copy.start()
        build_right(slot)
        for z, x in own:
            build_left(slot, z, x, False)
        for p in range(4):
            for t in range(2):
                add_pairs(p, t, [5, 6, 9, 10], True)
        for copy in copies[:NEAR]:
            copy.wait_recv()
        for z in (1, 2):
            for x in range(4):
                build_left(slot, z, x, True)
        for p in range(4):
            az, ax = p // 2, p % 2
            x = 3 * ax
            for t in range(2):
                add_pairs(p, t, [4 + x, 8 + x], False)
            add_pairs(p, 2, [4 * z + ax + i for z in (1, 2) for i in range(3)], True)
        for copy in copies[NEAR:]:
            copy.wait_recv()
        for z in (0, 3):
            for x in range(4):
                build_left(slot, z, x, True)
        for p in range(4):
            az, ax = p // 2, p % 2
            for t in range(3):
                add_pairs(p, t, [12 * az + ax + i for i in range(3)], False)
        update(slot)
        for copy in copies:
            copy.wait_send()
        return carry

    static_parts()
    pl.semaphore_wait(barrier, len(greeted))
    lax.fori_loop(0, STEPS, one_step, 0)

    myself = (me_z * n_x + me_x) * n_y + me_y
    states, seats = [], []
    for cell in range(8):
        z, x, y = cell // 4, cell // 2 % 2, cell % 2
        moved = jnp.concatenate(
            [region[STEPS, 1 + z, 1 + x, y], speed[cell // 2, 4 * y : 4 * y + 4]], axis=0
        )
        live = jnp.broadcast_to(live_ref[pl.ds(cell, 1), :], (8, ATOMS))
        states.append(jnp.where(is_xyz, moved * live, 0.0))
        seats.append(dest_ref[z, x, y])
    moves = []
    for r, d in enumerate(peers):
        target = device(d)
        base = ((target[0] * n_x + target[1]) * n_y + target[2]) * SEATS
        message = jnp.where(row8 == 3, -1.0, 0.0)
        for cell in range(8):
            seat = seats[cell] - base
            hit = jnp.logical_and(seat >= 0, seat < SEATS)
            tagged = jnp.where(row8 == 3, seat.astype(F32), states[cell])
            message = jnp.where(hit, tagged, message)
        send_box[r] = message
        move = pltpu.make_async_remote_copy(
            src_ref=send_box.at[r],
            dst_ref=box.at[r],
            send_sem=move_send_sem.at[r],
            recv_sem=move_recv_sem.at[r],
            device_id=target,
            device_id_type=MESH,
        )
        move.start()
        moves.append(move)
    results = []
    for seat in range(SEATS):
        result = zero8
        for cell in range(8):
            result = jnp.where(seats[cell] == myself * SEATS + seat, states[cell], result)
        results.append(result)
    for move in moves:
        move.wait_recv()
    messages = [box[r] for r in range(7)]
    marks = [jnp.broadcast_to(m[3:4], (8, ATOMS)) for m in messages]
    for seat in range(SEATS):
        result = results[seat]
        for r in range(7):
            result = jnp.where(marks[r] == float(seat), messages[r], result)
        for k in range(3):
            out_pos_ref[k, pl.ds(seat, 1), :] = result[k : k + 1]
            out_vel_ref[k, pl.ds(seat, 1), :] = result[4 + k : 5 + k]
    for move in moves:
        move.wait_send()


def on_device(positions, velocities, types, strength, counts, pair_list, destination):
    vmem = pl.BlockSpec(memory_space=pltpu.VMEM)
    smem = pl.BlockSpec(memory_space=pltpu.SMEM)
    shape = jax.ShapeDtypeStruct((3, SEATS, ATOMS), F32)
    return pl.pallas_call(
        body,
        out_shape=(shape, shape),
        in_specs=[vmem, vmem, vmem, smem, smem, smem, smem],
        out_specs=(vmem, vmem),
        scratch_shapes=[
            pltpu.VMEM((STEPS + 1, 4, 4, 4, 4, ATOMS), F32),
            pltpu.VMEM((4, 8, ATOMS), F32),
            pltpu.VMEM((8, ATOMS), F32),
            pltpu.VMEM((16, 32, ATOMS), BF16),
            pltpu.VMEM((16, ATOMS, DEPTH), BF16),
            pltpu.VMEM((4, 3, DEPTH, 2 * ATOMS), BF16),
            pltpu.VMEM((2, 16, 16 * ATOMS), BF16),
            pltpu.VMEM((4, 3, 16, 2 * ATOMS), F32),
            pltpu.VMEM((7, 8, ATOMS), F32),
            pltpu.VMEM((7, 8, ATOMS), F32),
            pltpu.SemaphoreType.DMA((STEPS, 26)),
            pltpu.SemaphoreType.DMA((STEPS, 26)),
            pltpu.SemaphoreType.DMA((7,)),
            pltpu.SemaphoreType.DMA((7,)),
        ],
        compiler_params=pltpu.CompilerParams(collective_id=0, has_side_effects=True),
    )(positions, velocities, types, strength, counts, pair_list, destination)


def solution(mesh):
    return jax.shard_map(
        on_device,
        mesh=mesh,
        in_specs=(
            P(None, "tower", "px", "py", None),
            P(None, "tower", "px", "py", None),
            P("tower", "px", "py", None),
            P(),
            P("tower", "px", "py"),
            P(None, "tower", "px", "py"),
            P("tower", "px", "py"),
        ),
        out_specs=(P(None, ("tower", "px", "py"), None), P(None, ("tower", "px", "py"), None)),
        check_vma=False,
    )
```

profile of v0, /device:TPU:1, one launch (start us, length us, event | category | flops | bytes accessed | tf_op | source)
XLA Modules:
  0.0 63.6 jit_solution(14814197149240694235)
XLA Ops:
  0.6 1.4 %copy.9.pair_ref = s32[27,2,2,2]{3,2,1,0:T(2,128)} copy(s32[27,2,2,2]{0,3,2,1:T(2,128)} %param.12) | data formatting | bytes 1728 | tf_op args[5]
  2.0 59.5 %shard_map.86 = (f32[3,15,128]{2,1,0:T(8,128)}, f32[3,15,128]{2,1,0:T(8,128)}) custom-call(f32[3,2,2,2,128]{4,3,2,1,0:T(2,128)} %pos_ref.1, f32[3,2,2,2,128]{4,3,2,1,0:T(2,128)} %vel_ref.1, s32[2,2,2,128]{3,2,1,0:T(2,128)} %types_ref.1, f32[16]{0:T(128)} %strength_ref.1, s32[2,2,2]{2,1,0:T(2,128)} %counts_ref.1, s32[27,2,2,2]{3,2,1,0:T(2,128)} %copy.9.pair_ref, ...), custom_call_target="tpu_custom_call" | custom-call | tf_op jit(solution)/shard_map/pallas_call | solution.py:359
  61.6 0.0 copy-start
  61.6 1.4 %copy.12 = f32[3,15,128]{2,1,0:T(8,128)} copy(f32[3,15,128]{2,1,0:T(8,128)} %get-tuple-element.4) | data formatting | bytes 46080
  62.9 0.0 copy-done
  62.9 0.6 copy.13
Async XLA Ops:
  61.6 1.4 %copy-start = (f32[3,15,128]{2,1,0:T(8,128)S(1)}, f32[3,15,128]{2,1,0:T(8,128)}, u32[]{:S(2)}) copy-start(f32[3,15,128]{2,1,0:T(8,128)} %get-tuple-element.5) | copy-start | bytes 69124
where the time goes:
time: 63.8 us; the launch traced here: 63.6 us
  Pallas kernels  59.5 us (93%)
  local copies, waits for them, and re-layouts  3.37 us (5%)
  between operations  0.65 us (1%)
    pallas_call x1, Pallas kernels, on_device(): pl.pallas_call(body, out_shape=(shape, shape), in_specs=[vmem, vmem, vmem...  59.5 us
    unnamed x5, local copies, waits for them, and re-layouts  3.37 us

commit v1 on v0

--- a/solution.py
+++ b/solution.py
@@ -12,7 +12,7 @@
 KINDS = 16
 SEATS = 15
 ATOMS = 128
-DEPTH = 192
+DEPTH = 176
 MESH = pl.DeviceIdType.MESH
 F32 = jnp.float32
 BF16 = jnp.bfloat16
@@ -48,29 +48,60 @@
     return jnp.concatenate([x[4:], x[:4]], axis=0)
 
 
+def host_of(t, x, y):
+    return (2 * (t // 2) + y // 4, x, 2 * lax.rem(y, 4) + lax.rem(t, 2))
+
+
 def body(
     pos_ref, vel_ref, types_ref, strength_ref, counts_ref, pair_ref, dest_ref,
     out_pos_ref, out_vel_ref,
-    region, speed, live_ref, flag_ref, left_ref, right_ref, value_ref, total, box, send_box,
-    send_sem, recv_sem, move_send_sem, move_recv_sem,
+    region, speed, seat_ref, parcel, hosted, flag_ref, left_ref, right_ref, value_ref, total,
+    box, stay_box, send_box, stay_send,
+    send_sem, recv_sem, host_sem, move_send_sem, move_recv_sem,
 ):
-    me_z, me_x, me_y = (lax.axis_index(a) for a in ("tower", "px", "py"))
+    home_t, home_x, home_y = (lax.axis_index(a) for a in ("tower", "px", "py"))
     n_z, n_x, n_y = (lax.axis_size(a) for a in ("tower", "px", "py"))
+    me_z = 2 * (home_t // 2) + lax.rem(home_y, 2)
+    me_x = home_x
+    me_y = 4 * lax.rem(home_t, 2) + home_y // 2
+    host = host_of(home_t, home_x, home_y)
+    same_tower = me_z == home_t
+    at_home = jnp.logical_and(same_tower, me_y == home_y)
 
     def device(d):
-        return (
+        return host_of(
             lax.rem(me_z + d[0] + n_z, n_z),
             lax.rem(me_x + d[1] + n_x, n_x),
             lax.rem(me_y + d[2] + n_y, n_y),
         )
 
-    peers = [(0, 0, r) for r in range(1, 8)]
-    greeted = DIRECTIONS + [p for p in peers if p[2] not in (1, 7)]
+    def shift_y(y, r):
+        return lax.rem(y + r + n_y, n_y)
+
+    def goes_to_itself(r):
+        return jnp.logical_and(same_tower, shift_y(me_y, r) == home_y)
+
     barrier = pltpu.get_barrier_semaphore()
-    for d in greeted:
-        pl.semaphore_signal(barrier, inc=1, device_id=device(d), device_id_type=MESH)
+
+    def greet(target):
+        pl.semaphore_signal(barrier, inc=1, device_id=target, device_id_type=MESH)
+
+    @pl.when(jnp.logical_not(at_home))
+    def _():
+        greet((me_z, me_x, me_y))
+
+    for d in DIRECTIONS:
+        greet(device(d))
+    for r in range(8):
+
+        @pl.when(jnp.logical_not(goes_to_itself(r)))
+        def _():
+            greet(host_of(home_t, home_x, shift_y(home_y, -r)))
+
+    expected = len(DIRECTIONS) + 9 - at_home.astype(jnp.int32) - same_tower.astype(jnp.int32)
 
     row8 = lax.broadcasted_iota(jnp.int32, (8, ATOMS), 0)
+    row16 = lax.broadcasted_iota(jnp.int32, (16, ATOMS), 0)
     low = row8 < 4
     comp = lax.rem(row8, 4)
     is_xyz = comp < 3
@@ -81,15 +112,25 @@
     for kind in range(KINDS):
         table = jnp.where(kinds == kind, strength_ref[kind], table)
     lanes = lax.broadcasted_iota(jnp.int32, (1, ATOMS), 1)
+    parcel[8] = zero8
     for cell in range(8):
         z, x, y = cell // 4, cell // 2 % 2, cell % 2
         live = (lanes < counts_ref[z, x, y]).astype(F32)
-        live_ref[pl.ds(cell, 1), :] = live
         for k in range(3):
-            region[0, 1 + z, 1 + x, y, pl.ds(k, 1), :] = pos_ref[k, z, x, pl.ds(y, 1), :]
-            speed[cell // 2, pl.ds(4 * y + k, 1), :] = vel_ref[k, z, x, pl.ds(y, 1), :]
-        region[0, 1 + z, 1 + x, y, pl.ds(3, 1), :] = table[cell : cell + 1] * live
-        speed[cell // 2, pl.ds(4 * y + 3, 1), :] = jnp.zeros((1, ATOMS), F32)
+            parcel[cell, pl.ds(k, 1), :] = pos_ref[k, z, x, pl.ds(y, 1), :]
+            parcel[cell, pl.ds(4 + k, 1), :] = vel_ref[k, z, x, pl.ds(y, 1), :]
+        parcel[cell, pl.ds(3, 1), :] = table[cell : cell + 1] * live
+        seat = dest_ref[z, x, y].astype(F32)
+        parcel[cell, pl.ds(7, 1), :] = jnp.full((1, ATOMS), seat, F32)
+        parcel[8, pl.ds(cell, 1), pl.ds(0, 27)] = pair_ref[z, x, pl.ds(y, 1), :].astype(F32)
+    delivery = pltpu.make_async_remote_copy(
+        src_ref=parcel,
+        dst_ref=hosted,
+        send_sem=host_sem.at[0],
+        recv_sem=host_sem.at[1],
+        device_id=host,
+        device_id_type=MESH,
+    )
 
     def halo_copies(slot):
         copies = []
@@ -107,36 +148,40 @@
             )
         return copies
 
-    def static_parts():
-        for z, x in itertools.product(range(4), range(4)):
-            tiles = []
-            for y in (0, 1, -1, 2):
-                tile = zero8
-                for cell in range(8):
-                    o = (z - 1 - cell // 4, x - 1 - cell // 2 % 2, y - cell % 2)
-                    if max(map(abs, o)) <= 1:
-                        k = (o[0] + 1) * 9 + (o[1] + 1) * 3 + o[2] + 1
-                        flag = pair_ref[k, cell // 4, cell // 2 % 2, cell % 2]
-                        tile = jnp.where(row8 == cell, (flag.astype(F32) - 1.0) * 100.0, tile)
-                tiles.append(tile)
-            flag_ref[4 * z + x] = jnp.concatenate(tiles, axis=0).astype(BF16)
+    def constant_parts():
         for p in range(4):
             for t in range(3):
                 for side in range(2):
                     half = ((0, 0), (1, 1), (0, 1))[t][side]
                     mark = jnp.where((low if half == 0 else ~low) & is_xyz, -1.0, 0.0)
                     pair = [mark, zero8] if t < 2 else [zero8, mark]
-                    seat = ((0, 0), (1, 1), (2, 3))[t][side]
-                    picks = [
-                        jnp.where(row8 == 2 * p + side, 1.0, 0.0) if s == seat else zero8
-                        for s in range(4)
-                    ]
                     right_ref[p, t, 96:144, pl.ds(128 * side, 128)] = jnp.concatenate(
                         pair * 3, axis=0
                     ).astype(BF16)
-                    right_ref[p, t, 160:192, pl.ds(128 * side, 128)] = jnp.concatenate(
-                        picks, axis=0
-                    ).astype(BF16)
+
+    def unpack():
+        for cell in range(8):
+            z, x, y = cell // 4, cell // 2 % 2, cell % 2
+            tile = hosted[cell]
+            region[0, 1 + z, 1 + x, y] = tile[:4]
+            speed[cell // 2, pl.ds(4 * y, 4), :] = jnp.where(row8[:4] < 3, tile[4:], 0.0)
+            seat_ref[cell] = jnp.broadcast_to(tile[7:8], (8, ATOMS))
+        padded = jnp.concatenate([(hosted[8] - 1.0) * 100.0] + [zero8] * 15, axis=0)
+        turned = padded.T
+        for cell in range(8):
+            flag_ref[cell] = jnp.broadcast_to(turned[:32, cell : cell + 1], (32, ATOMS))
+        for p, side in itertools.product(range(4), range(2)):
+            cell, z, x = 2 * p + side, p // 2, p % 2
+            rows32 = flag_ref[cell]
+            for t in range(3):
+                y = ((0, 0), (1, 1), (-1, 2))[t][side] - side + 1
+                rows = [jnp.zeros((1, ATOMS), F32)] * 16
+                for oz, ox in itertools.product(range(3), range(3)):
+                    k = 9 * oz + 3 * ox + y
+                    rows[4 * (z + oz) + x + ox] = rows32[k : k + 1]
+                right_ref[p, t, 160:176, pl.ds(128 * side, 128)] = jnp.concatenate(
+                    rows, axis=0
+                ).astype(BF16)
 
     def shift_of(z, x, part):
         y_low, y_high = ((-1.0, 0.0), (-2.0, 1.0))[part]
@@ -177,11 +222,8 @@
         rows = []
         for kind in (0, 0, 1, 1, 0, 2, 3, 4, 5):
             rows += [parts[0][kind], parts[1][kind]]
-        rows += [jnp.ones((16, ATOMS), F32)]
-        stack = jnp.concatenate(
-            [jnp.concatenate(rows, axis=0).astype(BF16), flag_ref[column]], axis=0
-        )
-        left_ref[column] = stack.T
+        rows += [jnp.ones((16, ATOMS), F32), jnp.where(row16 == column, 1.0, 0.0)]
+        left_ref[column] = jnp.concatenate(rows, axis=0).astype(BF16).T
 
     def build_right(slot):
         for p in range(4):
@@ -296,60 +338,82 @@
             copy.wait_send()
         return carry
 
-    static_parts()
-    pl.semaphore_wait(barrier, len(greeted))
+    constant_parts()
+    pl.semaphore_wait(barrier, expected)
+
+    @pl.when(jnp.logical_not(at_home))
+    def _():
+        delivery.start()
+        delivery.wait_recv()
+        delivery.wait_send()
+
+    @pl.when(at_home)
+    def _():
+        hosted[...] = parcel[...]
+
+    unpack()
     lax.fori_loop(0, STEPS, one_step, 0)
 
-    myself = (me_z * n_x + me_x) * n_y + me_y
-    states, seats = [], []
+    states, moves = [], []
     for cell in range(8):
         z, x, y = cell // 4, cell // 2 % 2, cell % 2
-        moved = jnp.concatenate(
-            [region[STEPS, 1 + z, 1 + x, y], speed[cell // 2, 4 * y : 4 * y + 4]], axis=0
-        )
-        live = jnp.broadcast_to(live_ref[pl.ds(cell, 1), :], (8, ATOMS))
-        states.append(jnp.where(is_xyz, moved * live, 0.0))
-        seats.append(dest_ref[z, x, y])
-    moves = []
-    for r, d in enumerate(peers):
-        target = device(d)
-        base = ((target[0] * n_x + target[1]) * n_y + target[2]) * SEATS
+        here = region[STEPS, 1 + z, 1 + x, y]
+        moved = jnp.concatenate([here, speed[cell // 2, 4 * y : 4 * y + 4]], axis=0)
+        live = jnp.broadcast_to(here[3:4], (8, ATOMS)) > 0.0
+        states.append(jnp.where(live & is_xyz, moved, 0.0))
+    for r in range(8):
+        y = shift_y(me_y, r)
+        base = (((me_z * n_x + me_x) * n_y + y) * SEATS).astype(F32)
         message = jnp.where(row8 == 3, -1.0, 0.0)
         for cell in range(8):
-            seat = seats[cell] - base
-            hit = jnp.logical_and(seat >= 0, seat < SEATS)
-            tagged = jnp.where(row8 == 3, seat.astype(F32), states[cell])
-            message = jnp.where(hit, tagged, message)
-        send_box[r] = message
+            seat = seat_ref[cell] - base
+            hit = (seat >= 0.0) & (seat < float(SEATS))
+            tagged = jnp.where(row8 == 3, seat, states[cell])
+            if r == 0:
+                stay_send[cell] = jnp.where(hit, tagged, jnp.where(row8 == 3, -1.0, 0.0))
+            else:
+                message = jnp.where(hit, tagged, message)
+        if r > 0:
+            send_box[r - 1] = message
+        src, dst = (stay_send, stay_box) if r == 0 else (send_box.at[r - 1], box.at[r - 1])
         move = pltpu.make_async_remote_copy(
-            src_ref=send_box.at[r],
-            dst_ref=box.at[r],
+            src_ref=src,
+            dst_ref=dst,
             send_sem=move_send_sem.at[r],
             recv_sem=move_recv_sem.at[r],
-            device_id=target,
+            device_id=(me_z, me_x, y),
             device_id_type=MESH,
         )
-        move.start()
         moves.append(move)
-    results = []
+
+        @pl.when(jnp.logical_not(goes_to_itself(r)))
+        def _():
+            move.start()
+
+        @pl.when(goes_to_itself(r))
+        def _():
+            dst[...] = src[...]
+
+    for r in range(8):
+
+        @pl.when(jnp.logical_not(goes_to_itself(r)))
+        def _():
+            moves[r].wait_recv()
+
+    messages = [stay_box[cell] for cell in range(8)] + [box[r] for r in range(7)]
+    marks = [jnp.broadcast_to(m[3:4], (8, ATOMS)) for m in messages]
     for seat in range(SEATS):
         result = zero8
-        for cell in range(8):
-            result = jnp.where(seats[cell] == myself * SEATS + seat, states[cell], result)
-        results.append(result)
-    for move in moves:
-        move.wait_recv()
-    messages = [box[r] for r in range(7)]
-    marks = [jnp.broadcast_to(m[3:4], (8, ATOMS)) for m in messages]
-    for seat in range(SEATS):
-        result = results[seat]
-        for r in range(7):
-            result = jnp.where(marks[r] == float(seat), messages[r], result)
+        for mark, message in zip(marks, messages):
+            result = jnp.where(mark == float(seat), message, result)
         for k in range(3):
             out_pos_ref[k, pl.ds(seat, 1), :] = result[k : k + 1]
             out_vel_ref[k, pl.ds(seat, 1), :] = result[4 + k : 5 + k]
-    for move in moves:
-        move.wait_send()
+    for r in range(8):
+
+        @pl.when(jnp.logical_not(goes_to_itself(r)))
+        def _():
+            moves[r].wait_send()
 
 
 def on_device(positions, velocities, types, strength, counts, pair_list, destination):
@@ -359,26 +423,31 @@
     return pl.pallas_call(
         body,
         out_shape=(shape, shape),
-        in_specs=[vmem, vmem, vmem, smem, smem, smem, smem],
+        in_specs=[vmem, vmem, vmem, smem, smem, vmem, smem],
         out_specs=(vmem, vmem),
         scratch_shapes=[
             pltpu.VMEM((STEPS + 1, 4, 4, 4, 4, ATOMS), F32),
             pltpu.VMEM((4, 8, ATOMS), F32),
-            pltpu.VMEM((8, ATOMS), F32),
-            pltpu.VMEM((16, 32, ATOMS), BF16),
+            pltpu.VMEM((8, 8, ATOMS), F32),
+            pltpu.VMEM((9, 8, ATOMS), F32),
+            pltpu.VMEM((9, 8, ATOMS), F32),
+            pltpu.VMEM((8, 32, ATOMS), F32),
             pltpu.VMEM((16, ATOMS, DEPTH), BF16),
             pltpu.VMEM((4, 3, DEPTH, 2 * ATOMS), BF16),
             pltpu.VMEM((2, 16, 16 * ATOMS), BF16),
             pltpu.VMEM((4, 3, 16, 2 * ATOMS), F32),
             pltpu.VMEM((7, 8, ATOMS), F32),
+            pltpu.VMEM((8, 8, ATOMS), F32),
             pltpu.VMEM((7, 8, ATOMS), F32),
+            pltpu.VMEM((8, 8, ATOMS), F32),
             pltpu.SemaphoreType.DMA((STEPS, 26)),
             pltpu.SemaphoreType.DMA((STEPS, 26)),
-            pltpu.SemaphoreType.DMA((7,)),
-            pltpu.SemaphoreType.DMA((7,)),
+            pltpu.SemaphoreType.DMA((2,)),
+            pltpu.SemaphoreType.DMA((8,)),
+            pltpu.SemaphoreType.DMA((8,)),
         ],
         compiler_params=pltpu.CompilerParams(collective_id=0, has_side_effects=True),
-    )(positions, velocities, types, strength, counts, pair_list, destination)
+    )(positions, velocities, types, strength, counts, pair_list.transpose(1, 2, 3, 0), destination)
 
 
 def solution(mesh):

time: 63.8 us -> 56.9 us (0.89)
  Pallas kernels: 59.5 us -> 54 us
  local copies, waits for them, and re-layouts: 3.37 us -> 1.96 us
    pallas_call x1, Pallas kernels: 59.5 us -> 54 us  [on_device(): pl.pallas_call(body, out_shape=(shape, shape), in_specs=[vmem, vmem, vmem...]
    unnamed x5 -> x4, local copies, waits for them, and re-layouts: 3.37 us -> 1.96 us
where the time goes in v1:
time: 56.9 us; the launch traced here: 56.7 us
  Pallas kernels  54 us (95%)
  local copies, waits for them, and re-layouts  1.96 us (3%)
  between operations  0.65 us (1%)
    pallas_call x1, Pallas kernels, on_device(): pl.pallas_call(body, out_shape=(shape, shape), in_specs=[vmem, vmem, vmem...  54 us
    unnamed x4, local copies, waits for them, and re-layouts  1.96 us

profile of v1, /device:TPU:1, one launch (start us, length us, event | category | flops | bytes accessed | tf_op | source)
XLA Modules:
  0.0 56.7 jit_solution(11599619057308906177)
XLA Ops:
  0.6 54.0 %shard_map.86 = (f32[3,15,128]{2,1,0:T(8,128)}, f32[3,15,128]{2,1,0:T(8,128)}) custom-call(f32[3,2,2,2,128]{4,3,2,1,0:T(2,128)} %pos_ref.1, f32[3,2,2,2,128]{4,3,2,1,0:T(2,128)} %vel_ref.1, s32[2,2,2,128]{3,2,1,0:T(2,128)} %types_ref.1, f32[16]{0:T(128)} %strength_ref.1, s32[2,2,2]{2,1,0:T(2,128)} %counts_ref.1, s32[2,2,2,27]{3,2,1,0:T(2,128)} %bitcast.1, ...), custom_call_target="tpu_custom_call" | custom-call | tf_op jit(solution)/shard_map/pallas_call | solution.py:423
  54.7 0.0 copy-start
  54.7 1.4 %copy.11 = f32[3,15,128]{2,1,0:T(8,128)} copy(f32[3,15,128]{2,1,0:T(8,128)} %get-tuple-element.4) | data formatting | bytes 46080
  56.0 0.0 copy-done
  56.1 0.6 %copy.12 = f32[3,15,128]{2,1,0:T(8,128)} copy(f32[3,15,128]{2,1,0:T(8,128)S(1)} %copy-done) | data formatting | bytes 46080
Async XLA Ops:
  54.7 1.4 %copy-start = (f32[3,15,128]{2,1,0:T(8,128)S(1)}, f32[3,15,128]{2,1,0:T(8,128)}, u32[]{:S(2)}) copy-start(f32[3,15,128]{2,1,0:T(8,128)} %get-tuple-element.5) | copy-start | bytes 69124

commit v2 on v1

--- a/solution.py
+++ b/solution.py
@@ -12,16 +12,17 @@
 KINDS = 16
 SEATS = 15
 ATOMS = 128
-DEPTH = 176
+DEPTH = 112
+CHUNK, AHEAD = 2, 2
 MESH = pl.DeviceIdType.MESH
 F32 = jnp.float32
 BF16 = jnp.bfloat16
 
 DIRECTIONS = sorted(
     (d for d in itertools.product((-1, 0, 1), repeat=3) if d != (0, 0, 0)),
-    key=lambda d: abs(d[0]),
+    key=lambda d: (sum(map(abs, d)), abs(d[1]) + abs(d[2])),
 )
-NEAR = 8
+NEAREST, FACES, EDGES = 2, 6, 18
 SEAT_OF_Y = {0: 0, 1: 1, -1: 2, 2: 3}
 
 
@@ -154,9 +155,8 @@
                 for side in range(2):
                     half = ((0, 0), (1, 1), (0, 1))[t][side]
                     mark = jnp.where((low if half == 0 else ~low) & is_xyz, -1.0, 0.0)
-                    pair = [mark, zero8] if t < 2 else [zero8, mark]
-                    right_ref[p, t, 96:144, pl.ds(128 * side, 128)] = jnp.concatenate(
-                        pair * 3, axis=0
+                    right_ref[p, 80:96, pl.ds(256 * t + 128 * side, 128)] = jnp.concatenate(
+                        [mark, mark], axis=0
                     ).astype(BF16)
 
     def unpack():
@@ -179,7 +179,7 @@
                 for oz, ox in itertools.product(range(3), range(3)):
                     k = 9 * oz + 3 * ox + y
                     rows[4 * (z + oz) + x + ox] = rows32[k : k + 1]
-                right_ref[p, t, 160:176, pl.ds(128 * side, 128)] = jnp.concatenate(
+                right_ref[p, 96:112, pl.ds(256 * t + 128 * side, 128)] = jnp.concatenate(
                     rows, axis=0
                 ).astype(BF16)
 
@@ -204,77 +204,82 @@
             axis=0,
         )
 
-    def build_left(slot, z, x, both):
+    def build_left(slot, z, x, part):
         column = 4 * z + x
-        parts = []
-        for part in range(2):
-            if part == 1 and not both:
-                parts.append([zero8] * 6)
-                continue
-            raw = own_tile(slot, z, x, part)
-            tile = raw + shift_of(z, x, part)
-            parts.append(list(thirds(tile)) + list(thirds(tile * tile)))
-            value = jnp.where(is_xyz, tile, 1.0) * strength_rows(raw)
-            high = value.astype(BF16).astype(F32)
-            value_ref[part, :, pl.ds(128 * column, 128)] = jnp.concatenate(
-                [high, value - high], axis=0
-            ).astype(BF16)
-        rows = []
-        for kind in (0, 0, 1, 1, 0, 2, 3, 4, 5):
-            rows += [parts[0][kind], parts[1][kind]]
-        rows += [jnp.ones((16, ATOMS), F32), jnp.where(row16 == column, 1.0, 0.0)]
-        left_ref[column] = jnp.concatenate(rows, axis=0).astype(BF16).T
+        raw = own_tile(slot, z, x, part)
+        tile = raw + shift_of(z, x, part)
+        high, mid, rest = thirds(tile)
+        ones = jnp.ones((24, ATOMS), F32)
+        rows = [high, high, mid, mid, high, rest, ones, *thirds(tile * tile)]
+        rows += [jnp.where(row16 == column, 1.0, 0.0)]
+        left_ref[part, column] = jnp.concatenate(rows, axis=0).astype(BF16).T
+        value = jnp.where(is_xyz, tile, 1.0) * strength_rows(raw)
+        high = value.astype(BF16).astype(F32)
+        value_ref[part, :, pl.ds(128 * column, 128)] = jnp.concatenate(
+            [high, value - high], axis=0
+        ).astype(BF16)
 
     def build_right(slot):
         for p in range(4):
             z, x = 1 + p // 2, 1 + p % 2
             tile = own_tile(slot, z, x, 0) + shift_of(z, x, 0)
             tile = jnp.where(is_xyz, tile, 0.0)
-            high, mid, rest = (2.0 * v for v in thirds(tile))
-            terms = [high, mid, high, mid, rest, high]
-            swapped = [swap_halves(v) for v in (high, mid, rest)]
-            swapped = [swapped[i] for i in (0, 1, 0, 1, 2, 0)]
+            terms = [2.0 * v for v in thirds(tile)]
+            swapped = [swap_halves(v) for v in terms]
             squares = [-v for v in thirds(tile * tile)]
-            squares_swapped = [swap_halves(v) for v in squares]
+            squares[0] = jnp.where(is_xyz, squares[0], 1.0)
             for side in range(2):
-                a, b = (squares, squares_swapped) if side == 0 else (squares_swapped, squares)
-                ones_rows = jnp.concatenate(
-                    [
-                        jnp.where(low, jnp.where(is_xyz, a[0], 1.0), b[1]),
-                        jnp.where(low, a[2], 0.0),
-                    ],
-                    axis=0,
-                ).astype(BF16)
+                mine = low if side == 0 else ~low
+                norms = [jnp.where(mine, v, 0.0) for v in squares]
                 for t in range(3):
                     half = ((0, 0), (1, 1), (0, 1))[t][side]
+                    keep = low if half == 0 else ~low
                     source = terms if half == side else swapped
-                    keep = low if half == 0 else ~low
-                    rows = []
-                    for v in source:
-                        v = jnp.where(keep, v, 0.0)
-                        rows += [v, zero8] if t < 2 else [zero8, v]
-                    at = pl.ds(128 * side, 128)
-                    right_ref[p, t, 0:96, at] = jnp.concatenate(rows, axis=0).astype(BF16)
-                    right_ref[p, t, 144:160, at] = ones_rows
-
-    def add_pairs(p, t, columns, first):
-        lhs = jnp.concatenate([left_ref[c] for c in columns], axis=0)
-        near = jnp.dot(lhs, right_ref[p, t], preferred_element_type=F32)
+                    high, mid, rest = [jnp.where(keep, v, 0.0) for v in source]
+                    mark = jnp.where(keep & is_xyz, -1.0, 0.0)
+                    rows = [high, mid, high, mid, rest, high, *norms, mark]
+                    right_ref[p, 0:80, pl.ds(256 * t + 128 * side, 128)] = jnp.concatenate(
+                        rows, axis=0
+                    ).astype(BF16)
+
+    def nearness(part, columns, targets):
+        lhs = jnp.concatenate([left_ref[part, c] for c in columns], axis=0)
+        rhs = jnp.concatenate(
+            [right_ref[p, :, pl.ds(256 * t, 256)] for p, t in targets], axis=1
+        )
+        return jnp.dot(lhs, rhs, preferred_element_type=F32)
+
+    def add_sums(near, part, columns, targets, first):
         near = jnp.maximum(near, 0.0)
         weight = near * near
         high = weight.astype(BF16)
         rest = (weight - high.astype(F32)).astype(BF16)
-        part = 0 if t < 2 else 1
         values = jnp.concatenate(
             [value_ref[part, :, pl.ds(128 * c, 128)] for c in columns], axis=1
         )
         add = jnp.dot(values, high, preferred_element_type=F32) + jnp.dot(
             values, rest, preferred_element_type=F32
         )
-        if first:
-            total[p, t] = add
-        else:
-            total[p, t] += add
+        for i, (p, t) in enumerate(targets):
+            more = add[:, 256 * i : 256 * i + 256]
+            if first:
+                total[p, t] = more
+            else:
+                total[p, t] += more
+
+    def add_pairs(groups):
+        parts = [
+            (part, columns[at : at + CHUNK], targets, first and at == 0)
+            for part, columns, targets, first in groups
+            for at in range(0, len(columns), CHUNK)
+        ]
+        waiting = []
+        for group in parts:
+            waiting.append((nearness(*group[:3]), *group))
+            if len(waiting) > AHEAD:
+                add_sums(*waiting.pop(0))
+        for group in waiting:
+            add_sums(*group)
 
     def update(slot):
         for p in range(4):
@@ -301,7 +306,10 @@
             region[slot + 1, z, x, 0] = new[:4]
             region[slot + 1, z, x, 1] = new[4:]
 
-    own = [(z, x) for z in (1, 2) for x in (1, 2)]
+    inner = (1, 2)
+    own = [(z, x) for z in inner for x in inner]
+    beside = [(z, x) for z in (0, 3) for x in inner] + [(z, x) for z in inner for x in (0, 3)]
+    across = [(z, x) for z in (0, 3) for x in (0, 3)]
 
     def one_step(slot, carry):
         copies = halo_copies(slot)
@@ -309,30 +317,54 @@
             copy.start()
         build_right(slot)
         for z, x in own:
-            build_left(slot, z, x, False)
-        for p in range(4):
-            for t in range(2):
-                add_pairs(p, t, [5, 6, 9, 10], True)
-        for copy in copies[:NEAR]:
-            copy.wait_recv()
-        for z in (1, 2):
-            for x in range(4):
-                build_left(slot, z, x, True)
-        for p in range(4):
-            az, ax = p // 2, p % 2
-            x = 3 * ax
-            for t in range(2):
-                add_pairs(p, t, [4 + x, 8 + x], False)
-            add_pairs(p, 2, [4 * z + ax + i for z in (1, 2) for i in range(3)], True)
-        for copy in copies[NEAR:]:
+            build_left(slot, z, x, 0)
+        add_pairs([(0, [5, 6, 9, 10], [(p, 0), (p, 1)], True) for p in range(4)])
+        for copy in copies[:NEAREST]:
             copy.wait_recv()
         for z in (0, 3):
-            for x in range(4):
-                build_left(slot, z, x, True)
-        for p in range(4):
-            az, ax = p // 2, p % 2
-            for t in range(3):
-                add_pairs(p, t, [12 * az + ax + i for i in range(3)], False)
+            for x in inner:
+                build_left(slot, z, x, 0)
+        add_pairs(
+            [
+                (0, [12 * (p // 2) + 1, 12 * (p // 2) + 2], [(p, 0), (p, 1)], False)
+                for p in range(4)
+            ]
+        )
+        for copy in copies[NEAREST:FACES]:
+            copy.wait_recv()
+        for z, x in own:
+            build_left(slot, z, x, 1)
+        for z in inner:
+            for x in (0, 3):
+                build_left(slot, z, x, 0)
+        add_pairs(
+            [(1, [5, 6, 9, 10], [(p, 2), (p + 1, 2)], True) for p in (0, 2)]
+            + [
+                (0, [4 + 3 * (p % 2), 8 + 3 * (p % 2)], [(p, 0), (p, 1)], False)
+                for p in range(4)
+            ]
+        )
+        for copy in copies[FACES:EDGES]:
+            copy.wait_recv()
+        for z, x in beside:
+            build_left(slot, z, x, 1)
+        for z, x in across:
+            build_left(slot, z, x, 0)
+        add_pairs(
+            [(1, [12 * i + 1, 12 * i + 2], [(2 * i, 2), (2 * i + 1, 2)], False) for i in (0, 1)]
+            + [(1, [4 + 3 * i, 8 + 3 * i], [(i, 2), (2 + i, 2)], False) for i in (0, 1)]
+            + [
+                (0, [12 * (p // 2) + 3 * (p % 2)], [(p, 0), (p, 1)], False)
+                for p in range(4)
+            ]
+        )
+        for copy in copies[EDGES:]:
+            copy.wait_recv()
+        for z, x in across:
+            build_left(slot, z, x, 1)
+        add_pairs(
+            [(1, [12 * (p // 2) + 3 * (p % 2)], [(p, 2)], False) for p in range(4)]
+        )
         update(slot)
         for copy in copies:
             copy.wait_send()
@@ -432,8 +464,8 @@
             pltpu.VMEM((9, 8, ATOMS), F32),
             pltpu.VMEM((9, 8, ATOMS), F32),
             pltpu.VMEM((8, 32, ATOMS), F32),
-            pltpu.VMEM((16, ATOMS, DEPTH), BF16),
-            pltpu.VMEM((4, 3, DEPTH, 2 * ATOMS), BF16),
+            pltpu.VMEM((2, 16, ATOMS, DEPTH), BF16),
+            pltpu.VMEM((4, DEPTH, 6 * ATOMS), BF16),
             pltpu.VMEM((2, 16, 16 * ATOMS), BF16),
             pltpu.VMEM((4, 3, 16, 2 * ATOMS), F32),
             pltpu.VMEM((7, 8, ATOMS), F32),

time: 56.9 us -> 52.3 us (0.919)
  Pallas kernels: 54 us -> 49.5 us
    pallas_call x1, Pallas kernels: 54 us -> 49.5 us  [on_device(): pl.pallas_call(body, out_shape=(shape, shape), in_specs=[vmem, vmem, vmem...]
where the time goes in v2:
time: 52.3 us; the launch traced here: 52.1 us
  Pallas kernels  49.5 us (95%)
  local copies, waits for them, and re-layouts  1.96 us (4%)
  between operations  0.65 us (1%)
    pallas_call x1, Pallas kernels, on_device(): pl.pallas_call(body, out_shape=(shape, shape), in_specs=[vmem, vmem, vmem...  49.5 us
    unnamed x4, local copies, waits for them, and re-layouts  1.96 us

profile of v2, /device:TPU:1, one launch (start us, length us, event | category | flops | bytes accessed | tf_op | source)
XLA Modules:
  0.0 52.1 jit_solution(5363373774277799112)
XLA Ops:
  0.6 49.5 %shard_map.86 = (f32[3,15,128]{2,1,0:T(8,128)}, f32[3,15,128]{2,1,0:T(8,128)}) custom-call(f32[3,2,2,2,128]{4,3,2,1,0:T(2,128)} %pos_ref.1, f32[3,2,2,2,128]{4,3,2,1,0:T(2,128)} %vel_ref.1, s32[2,2,2,128]{3,2,1,0:T(2,128)} %types_ref.1, f32[16]{0:T(128)} %strength_ref.1, s32[2,2,2]{2,1,0:T(2,128)} %counts_ref.1, s32[2,2,2,27]{3,2,1,0:T(2,128)} %bitcast.1, ...), custom_call_target="tpu_custom_call" | custom-call | tf_op jit(solution)/shard_map/pallas_call | solution.py:455
  50.1 0.0 copy-start
  50.1 1.4 %copy.11 = f32[3,15,128]{2,1,0:T(8,128)} copy(f32[3,15,128]{2,1,0:T(8,128)} %get-tuple-element.4) | data formatting | bytes 46080
  51.5 0.0 copy-done
  51.5 0.6 %copy.12 = f32[3,15,128]{2,1,0:T(8,128)} copy(f32[3,15,128]{2,1,0:T(8,128)S(1)} %copy-done) | data formatting | bytes 46080
Async XLA Ops:
  50.1 1.4 %copy-start = (f32[3,15,128]{2,1,0:T(8,128)S(1)}, f32[3,15,128]{2,1,0:T(8,128)}, u32[]{:S(2)}) copy-start(f32[3,15,128]{2,1,0:T(8,128)} %get-tuple-element.5) | copy-start | bytes 69124

commit v3 on v2

--- a/solution.py
+++ b/solution.py
@@ -53,13 +53,24 @@
     return (2 * (t // 2) + y // 4, x, 2 * lax.rem(y, 4) + lax.rem(t, 2))
 
 
-def body(
-    pos_ref, vel_ref, types_ref, strength_ref, counts_ref, pair_ref, dest_ref,
-    out_pos_ref, out_vel_ref,
+def body(*refs):
+    inputs, (out_pos_ref, out_vel_ref), local = refs[:7], refs[7:9], refs[9:16]
+    program(inputs, local, out_pos_ref, out_vel_ref, *refs[16:])
+
+
+def program(
+    inputs, local, out_pos_ref, out_vel_ref, load_sem,
     region, speed, seat_ref, parcel, hosted, flag_ref, left_ref, right_ref, value_ref, total,
     box, stay_box, send_box, stay_send,
     send_sem, recv_sem, host_sem, move_send_sem, move_recv_sem,
 ):
+    pos_ref, vel_ref, types_ref, strength_ref, counts_ref, pair_ref, dest_ref = local
+    loads = [
+        pltpu.make_async_copy(source, target, load_sem.at[i])
+        for i, (source, target) in enumerate(zip(inputs, local))
+    ]
+    for load in loads:
+        load.start()
     home_t, home_x, home_y = (lax.axis_index(a) for a in ("tower", "px", "py"))
     n_z, n_x, n_y = (lax.axis_size(a) for a in ("tower", "px", "py"))
     me_z = 2 * (home_t // 2) + lax.rem(home_y, 2)
@@ -107,6 +118,9 @@
     comp = lax.rem(row8, 4)
     is_xyz = comp < 3
     zero8 = jnp.zeros((8, ATOMS), F32)
+
+    for load in loads:
+        load.wait()
 
     kinds = types_ref[...].reshape(8, ATOMS)
     table = jnp.zeros((8, ATOMS), F32)
@@ -450,14 +464,21 @@
 
 def on_device(positions, velocities, types, strength, counts, pair_list, destination):
     vmem = pl.BlockSpec(memory_space=pltpu.VMEM)
-    smem = pl.BlockSpec(memory_space=pltpu.SMEM)
-    shape = jax.ShapeDtypeStruct((3, SEATS, ATOMS), F32)
+    shape = pltpu.VMEM((3, SEATS, ATOMS), F32)
     return pl.pallas_call(
         body,
         out_shape=(shape, shape),
-        in_specs=[vmem, vmem, vmem, smem, smem, vmem, smem],
+        in_specs=[pl.BlockSpec(memory_space=pl.ANY)] * 7,
         out_specs=(vmem, vmem),
         scratch_shapes=[
+            pltpu.VMEM((3, 2, 2, 2, ATOMS), F32),
+            pltpu.VMEM((3, 2, 2, 2, ATOMS), F32),
+            pltpu.VMEM((2, 2, 2, ATOMS), jnp.int32),
+            pltpu.SMEM((KINDS,), F32),
+            pltpu.SMEM((2, 2, 2), jnp.int32),
+            pltpu.VMEM((2, 2, 2, 27), jnp.int32),
+            pltpu.SMEM((2, 2, 2), jnp.int32),
+            pltpu.SemaphoreType.DMA((7,)),
             pltpu.VMEM((STEPS + 1, 4, 4, 4, 4, ATOMS), F32),
             pltpu.VMEM((4, 8, ATOMS), F32),
             pltpu.VMEM((8, 8, ATOMS), F32),

time: 52.3 us -> 50 us (0.956)
  Pallas kernels: 49.5 us -> 48 us
  local copies, waits for them, and re-layouts: 1.96 us -> 1.22 us
    pallas_call x1, Pallas kernels: 49.5 us -> 48 us  [on_device(): pl.pallas_call(body, out_shape=(shape, shape), in_specs=[pl.BlockSpec(mem...]
    unnamed x4 -> x2, local copies, waits for them, and re-layouts: 1.96 us -> 1.22 us
where the time goes in v3:
time: 50 us; the launch traced here: 49.9 us
  Pallas kernels  48 us (96%)
  local copies, waits for them, and re-layouts  1.22 us (2%)
  between operations  0.64 us (1%)
    pallas_call x1, Pallas kernels, on_device(): pl.pallas_call(body, out_shape=(shape, shape), in_specs=[pl.BlockSpec(mem...  48 us
    unnamed x2, local copies, waits for them, and re-layouts  1.22 us

profile of v3, /device:TPU:1, one launch (start us, length us, event | category | flops | bytes accessed | tf_op | source)
XLA Modules:
  0.0 49.9 jit_solution(13626986075207886916)
XLA Ops:
  0.6 48.0 %shard_map.86 = (f32[3,15,128]{2,1,0:T(8,128)S(1)}, f32[3,15,128]{2,1,0:T(8,128)S(1)}) custom-call(f32[3,2,2,2,128]{4,3,2,1,0:T(2,128)} %refs_0_.1, f32[3,2,2,2,128]{4,3,2,1,0:T(2,128)} %refs_1_.1, s32[2,2,2,128]{3,2,1,0:T(2,128)} %refs_2_.1, f32[16]{0:T(128)} %refs_3_.1, s32[2,2,2]{2,1,0:T(2,128)} %refs_4_.1, s32[2,2,2,27]{3,2,1,0:T(2,128)} %bitcast.1, ...), custom_call_target="tpu_custom_call" | custom-call | tf_op jit(solution)/shard_map/pallas_call | solution.py:468
  48.7 0.6 %copy.11 = f32[3,15,128]{2,1,0:T(8,128)} copy(f32[3,15,128]{2,1,0:T(8,128)S(1)} %get-tuple-element.2) | data formatting | bytes 46080
  49.3 0.6 %copy.12 = f32[3,15,128]{2,1,0:T(8,128)} copy(f32[3,15,128]{2,1,0:T(8,128)S(1)} %get-tuple-element.3) | data formatting | bytes 46080

commit v4 on v3

--- a/solution.py
+++ b/solution.py
@@ -102,8 +102,9 @@
     def _():
         greet((me_z, me_x, me_y))
 
-    for d in DIRECTIONS:
-        greet(device(d))
+    targets = [device(d) for d in DIRECTIONS]
+    for target in targets:
+        greet(target)
     for r in range(8):
 
         @pl.when(jnp.logical_not(goes_to_itself(r)))
@@ -157,7 +158,7 @@
                     dst_ref=region.at[slot, tz, tx, ty],
                     send_sem=send_sem.at[slot, i],
                     recv_sem=recv_sem.at[slot, i],
-                    device_id=device(d),
+                    device_id=targets[i],
                     device_id_type=MESH,
                 )
             )
@@ -344,6 +345,8 @@
                 for p in range(4)
             ]
         )
+        for copy in copies:
+            copy.wait_send()
         for copy in copies[NEAREST:FACES]:
             copy.wait_recv()
         for z, x in own:
@@ -380,8 +383,6 @@
             [(1, [12 * (p // 2) + 3 * (p % 2)], [(p, 2)], False) for p in range(4)]
         )
         update(slot)
-        for copy in copies:
-            copy.wait_send()
         return carry
 
     constant_parts()
@@ -444,6 +445,7 @@
 
         @pl.when(jnp.logical_not(goes_to_itself(r)))
         def _():
+            moves[r].wait_send()
             moves[r].wait_recv()
 
     messages = [stay_box[cell] for cell in range(8)] + [box[r] for r in range(7)]
@@ -455,11 +457,6 @@
         for k in range(3):
             out_pos_ref[k, pl.ds(seat, 1), :] = result[k : k + 1]
             out_vel_ref[k, pl.ds(seat, 1), :] = result[4 + k : 5 + k]
-    for r in range(8):
-
-        @pl.when(jnp.logical_not(goes_to_itself(r)))
-        def _():
-            moves[r].wait_send()
 
 
 def on_device(positions, velocities, types, strength, counts, pair_list, destination):

time: 50 us -> 49.9 us (level)
  no operation moved by 1% of the time
where the time goes in v4:
time: 49.9 us; the launch traced here: 49.8 us
  Pallas kernels  47.9 us (96%)
  local copies, waits for them, and re-layouts  1.22 us (2%)
  between operations  0.64 us (1%)
    pallas_call x1, Pallas kernels, on_device(): pl.pallas_call(body, out_shape=(shape, shape), in_specs=[pl.BlockSpec(mem...  47.9 us
    unnamed x2, local copies, waits for them, and re-layouts  1.22 us

profile of v4, /device:TPU:1, one launch (start us, length us, event | category | flops | bytes accessed | tf_op | source)
XLA Modules:
  0.0 49.8 jit_solution(6607816300947019714)
XLA Ops:
  0.6 47.9 %shard_map.86 = (f32[3,15,128]{2,1,0:T(8,128)S(1)}, f32[3,15,128]{2,1,0:T(8,128)S(1)}) custom-call(f32[3,2,2,2,128]{4,3,2,1,0:T(2,128)} %refs_0_.1, f32[3,2,2,2,128]{4,3,2,1,0:T(2,128)} %refs_1_.1, s32[2,2,2,128]{3,2,1,0:T(2,128)} %refs_2_.1, f32[16]{0:T(128)} %refs_3_.1, s32[2,2,2]{2,1,0:T(2,128)} %refs_4_.1, s32[2,2,2,27]{3,2,1,0:T(2,128)} %bitcast.1, ...), custom_call_target="tpu_custom_call" | custom-call | tf_op jit(solution)/shard_map/pallas_call | solution.py:465
  48.6 0.6 %copy.11 = f32[3,15,128]{2,1,0:T(8,128)} copy(f32[3,15,128]{2,1,0:T(8,128)S(1)} %get-tuple-element.2) | data formatting | bytes 46080
  49.2 0.6 %copy.12 = f32[3,15,128]{2,1,0:T(8,128)} copy(f32[3,15,128]{2,1,0:T(8,128)S(1)} %get-tuple-element.3) | data formatting | bytes 46080

commit v5 on v4

--- a/solution.py
+++ b/solution.py
@@ -181,6 +181,8 @@
             region[0, 1 + z, 1 + x, y] = tile[:4]
             speed[cell // 2, pl.ds(4 * y, 4), :] = jnp.where(row8[:4] < 3, tile[4:], 0.0)
             seat_ref[cell] = jnp.broadcast_to(tile[7:8], (8, ATOMS))
+
+    def unpack_flags():
         padded = jnp.concatenate([(hosted[8] - 1.0) * 100.0] + [zero8] * 15, axis=0)
         turned = padded.T
         for cell in range(8):
@@ -328,8 +330,9 @@
 
     def one_step(slot, carry):
         copies = halo_copies(slot)
-        for copy in copies:
+        for copy in copies[NEAREST:FACES] + copies[:NEAREST] + copies[FACES:]:
             copy.start()
+        pl.when(slot == 0)(unpack_flags)
         build_right(slot)
         for z, x in own:
             build_left(slot, z, x, 0)

time: 49.9 us -> 50 us (level)
  no operation moved by 1% of the time
where the time goes in v5:
time: 50 us; the launch traced here: 49.9 us
  Pallas kernels  48 us (96%)
  local copies, waits for them, and re-layouts  1.22 us (2%)
  between operations  0.64 us (1%)
    pallas_call x1, Pallas kernels, on_device(): pl.pallas_call(body, out_shape=(shape, shape), in_specs=[pl.BlockSpec(mem...  48 us
    unnamed x2, local copies, waits for them, and re-layouts  1.22 us

profile of v5, /device:TPU:1, one launch (start us, length us, event | category | flops | bytes accessed | tf_op | source)
XLA Modules:
  0.0 49.9 jit_solution(13771763184068387186)
XLA Ops:
  0.6 48.0 %shard_map.86 = (f32[3,15,128]{2,1,0:T(8,128)S(1)}, f32[3,15,128]{2,1,0:T(8,128)S(1)}) custom-call(f32[3,2,2,2,128]{4,3,2,1,0:T(2,128)} %refs_0_.1, f32[3,2,2,2,128]{4,3,2,1,0:T(2,128)} %refs_1_.1, s32[2,2,2,128]{3,2,1,0:T(2,128)} %refs_2_.1, f32[16]{0:T(128)} %refs_3_.1, s32[2,2,2]{2,1,0:T(2,128)} %refs_4_.1, s32[2,2,2,27]{3,2,1,0:T(2,128)} %bitcast.1, ...), custom_call_target="tpu_custom_call" | custom-call | tf_op jit(solution)/shard_map/pallas_call | solution.py:468
  48.6 0.6 %copy.11 = f32[3,15,128]{2,1,0:T(8,128)} copy(f32[3,15,128]{2,1,0:T(8,128)S(1)} %get-tuple-element.2) | data formatting | bytes 46080
  49.3 0.6 %copy.12 = f32[3,15,128]{2,1,0:T(8,128)} copy(f32[3,15,128]{2,1,0:T(8,128)S(1)} %get-tuple-element.3) | data formatting | bytes 46080
